TPU v7x, 32 devices: a whole 2x2x4 slice. The times are simulated.
32 devices in a mesh: seq: 8 (over z, x), head: 4 (over y, core).
Axes of the slice: x: 2, y: 2, z: 4, core: 2. Of those that a mesh axis runs over, the one named last changes fastest.
Arguments:
- xs: bfloat16 [8192, 4096], P('seq', 'head'), may hold values from -6 to 6
- gate_branch: bfloat16 [8192, 4096], P('seq', 'head'), may hold values from -6 to 6
- bmat: bfloat16 [8192, 128], P('seq'), may hold values from -0.375 to 0.375
- cmat: bfloat16 [8192, 128], P('seq'), may hold values from -0.375 to 0.375
- dt_code: int32 [64, 8192], P('head', 'seq'), may hold values from 1 to 32768
- resets: int32 [8192], P('seq'), may hold values 0 or 1
- decay_rate: float32 [64], P('head'), may hold values from 4.8828125e-05 to 0.08, as said below
- skip: float32 [64], P('head'), may hold values from 0.5 to 1.5
- norm_gain: float32 [4096], P('head'), may hold values from 0.1 to 1.9
- out_weight: bfloat16 [4096, 4096], P('head'), may hold values from -0.09375 to 0.09375
Outputs:
- mixed: bfloat16 [8192, 4096], P(('seq', 'head'))
Inputs may be any that keep to these rules, and one draw needn't show every extreme that they name: `decay_rate`: positive rates.
All inputs are finite; a program needn't handle non-finite values. No bound on the sum of `resets` on one device may be relied on, other than what follows from the above.
Results may differ from a plain program's by a relative error of at most 0.023.
Values may be sent and summed in bfloat16 or wider, within the bound.
No kernel may reach another device: no remote copies, remote signals or barrier semaphores. Data moves between devices by JAX's collectives and lax.ppermute only.
A program may use at most 128 MiB of HBM per device.

v0:
```python
import jax
import jax.numpy as jnp
from jax import lax
from jax.sharding import PartitionSpec as P

HEAD_DIM = 64
STATE = 128
SPAN = 256
INNER = 4096


def local(xs, gate_branch, bmat, cmat, dt_code, resets, decay_rate, skip, norm_gain, out_weight):
    tokens_here = xs.shape[0]
    local_heads = dt_code.shape[0]
    blocks = tokens_here // SPAN
    step_size = dt_code.astype(jnp.float32) / 16.0
    input_scale = jnp.minimum(step_size, 1.0)
    logarithmic_damping = -decay_rate[:, None] * step_size
    cumulative = jnp.cumsum(logarithmic_damping.reshape(local_heads, blocks, SPAN), axis=2)
    counts = jnp.cumsum(resets.reshape(blocks, SPAN), axis=1)
    position = jnp.arange(SPAN)
    linked = (counts[:, :, None] == counts[:, None, :]) & (position[None, :] <= position[:, None])[
        None
    ]
    gaps = jnp.where(linked[None], cumulative[:, :, :, None] - cumulative[:, :, None, :], 0.0)
    within = jnp.where(linked[None], jnp.exp(gaps), 0.0)
    key_blocks = bmat.reshape(blocks, SPAN, STATE)
    query_blocks = cmat.reshape(blocks, SPAN, STATE)
    intersection = jnp.einsum(
        "cin,cjn->cij", query_blocks, key_blocks, preferred_element_type=jnp.float32
    )
    raw_values = xs.reshape(blocks, SPAN, local_heads, HEAD_DIM)
    step_scale = input_scale.reshape(local_heads, blocks, SPAN).transpose(1, 2, 0)[:, :, :, None]
    scaled = (raw_values.astype(jnp.float32) * step_scale).astype(jnp.bfloat16)
    scores = (within * intersection[None]).astype(jnp.bfloat16)
    intra = jnp.einsum("hcij,cjhp->cihp", scores, scaled, preferred_element_type=jnp.float32)
    to_end = jnp.where(
        counts[None] == counts[None, :, -1:], jnp.exp(cumulative[:, :, -1:] - cumulative), 0.0
    )
    through = jnp.where(counts[None, :, -1] == 0, jnp.exp(cumulative[:, :, -1]), 0.0)
    from_start = jnp.where(counts[None] == 0, jnp.exp(cumulative), 0.0)
    weighted = (scaled.astype(jnp.float32) * to_end.transpose(1, 2, 0)[:, :, :, None]).astype(
        jnp.bfloat16
    )
    fresh = jnp.einsum("cjhp,cjn->chpn", weighted, key_blocks, preferred_element_type=jnp.float32)
    starts = []
    attained_limit = []
    running = jnp.zeros((local_heads, HEAD_DIM, STATE), jnp.float32)
    product = jnp.ones((local_heads,), jnp.float32)
    for block in range(blocks):
        starts.append(running)
        attained_limit.append(product)
        running = through[:, block, None, None] * running + fresh[block]
        product = product * through[:, block]
    local_starts = jnp.stack(starts)
    reach = jnp.stack(attained_limit, axis=0)
    query_float = query_blocks.astype(jnp.float32)
    start_weight = from_start.transpose(1, 2, 0)[:, :, :, None]
    decays = lax.all_gather(product[None], "seq", axis=0, tiled=True)
    shard_count = decays.shape[0]
    rank = lax.axis_index("seq")
    shard_ids = jnp.arange(shard_count)
    between = (shard_ids[None, :] > shard_ids[:, None]) & (shard_ids[None, :] < rank)
    factors = jnp.where(between[:, :, None], decays[None, :, :], 1.0)
    weights = jnp.prod(factors, axis=1) * (shard_ids < rank).astype(jnp.float32)[:, None]
    empty = jnp.zeros((local_heads, HEAD_DIM, STATE), jnp.float32)
    incoming = empty + jnp.einsum(
        "jh,jhpn->hpn",
        weights,
        lax.all_gather(running[None].astype(jnp.bfloat16), "seq", axis=0, tiled=True).astype(
            jnp.float32
        ),
        precision=lax.Precision.HIGHEST,
    )
    full_starts = local_starts + reach[:, :, None, None] * incoming[None]
    inter = (
        jnp.einsum("cin,chpn->cihp", query_float, full_starts, precision=lax.Precision.HIGHEST)
        * start_weight
    )
    result = intra + inter + skip[None, None, :, None] * raw_values.astype(jnp.float32)
    ssm_out = result.reshape(tokens_here, local_heads * HEAD_DIM)
    gated = ssm_out * jax.nn.silu(gate_branch.astype(jnp.float32))
    squared_values = lax.psum(jnp.sum(gated * gated, axis=1), "head")
    hidden = (
        gated * lax.rsqrt(squared_values[:, None] / INNER + 1e-05) * norm_gain[None, :]
    ).astype(jnp.bfloat16)
    return lax.psum_scatter(
        jnp.dot(hidden, out_weight, preferred_element_type=jnp.float32).astype(jnp.bfloat16),
        "head",
        scatter_dimension=0,
        tiled=True,
    )


def solution(mesh):
    in_specs = (
        P("seq", "head"),
        P("seq", "head"),
        P("seq", None),
        P("seq", None),
        P("head", "seq"),
        P("seq"),
        P("head"),
        P("head"),
        P("head"),
        P("head", None),
    )
    out_specs = P(("seq", "head"), None)
    return jax.shard_map(local, mesh=mesh, in_specs=in_specs, out_specs=out_specs, check_vma=False)
```

profile of v0, /device:TPU:0, one launch (start us, length us, event | category | flops | bytes accessed | tf_op | source)
XLA Modules:
  0.0 202.5 jit_solution(18144942277648591626)
XLA Ops:
  6.5 0.7 negate_multiply_fusion
  7.2 0.9 multiply_minimum_fusion
  8.2 0.1 reshape.267
  8.2 2.3 %reduce-window.16 = f32[16,4,2,128]{3,0,1,2:T(8,128)S(1)} reduce-window(f32[16,4,2,128]{3,0,1,2:T(8,128)S(1)} %copy.61, f32[]{:T(128)} %constant.12.clone.1), window={size=1x1x1x128 pad=0_0x0_0x0_0x127_0}, to_apply=%region_2.3 | reduce-window | flops 2080768 | bytes 131076 | tf_op jit(solution)/shard_map/reduce-window.2
  10.5 0.2 slice_reduce_fusion
  10.7 0.1 copy_bitcast_fusion
  10.8 0.2 slice_reduce_fusion.1
  11.0 2.3 %reduce-window.14 = s32[4,2,128]{2,1,0:T(2,128)S(1)} reduce-window(s32[4,2,128]{2,1,0:T(2,128)} %bitcast.105, s32[]{:T(128)} %constant.11.clone.1), window={size=1x1x128 pad=0_0x0_0x127_0}, to_apply=%region_0.0 | reduce-window | flops 130048 | bytes 8196 | tf_op jit(solution)/shard_map/reduce-window
  13.2 0.1 slice.62
  13.3 0.1 copy.59
  13.5 0.1 copy.60
  13.6 0.1 add_bitcast_fusion.1
  13.6 0.1 slice.65
  13.7 0.1 copy.75
  13.8 0.1 broadcast_compare_fusion
  13.9 0.1 select_bitcast_fusion
  14.1 4.1 %copy.58 = f32[1024,1024]{0,1:T(8,128)} copy(bf16[1024,1024]{1,0:T(8,128)(2,1)} %param.10) | data formatting | bytes 6291456 | tf_op jit(solution)/shard_map/convert_element_type | solution.py:34
  18.2 5.6 %reshape.272 = f32[4,256,16,64]{1,0,3,2:T(4,128)} reshape(f32[1024,1024]{0,1:T(8,128)} %copy.58) | data formatting | bytes 8388608 | tf_op jit(solution)/shard_map/convert_element_type | solution.py:34
  23.8 0.1 exponential_select_fusion
  23.9 0.6 slice_bitcast_fusion.3
  24.5 4.9 %multiply_convert_fusion.3 = (bf16[4,256,16,64]{1,0,3,2:T(4,128)(2,1)S(1)}, bf16[4,256,16,64]{1,0,3,2:T(4,128)(2,1)}) fusion(f32[4,256,16]{1,0,2:T(4,128)S(1)} %copy.65, f32[4,256,16,64]{1,0,3,2:T(4,128)} %reshape.272, f32[4,256,16]{1,0,2:T(4,128)S(1)} %bitcast.100), kind=kLoop, calls=%fused_computation.20 | loop fusion | flops 5242880 | bytes 8519680 | tf_op jit(solution)/shard_map/convert_element_type | solution.py:42
  29.4 0.7 fusion.20
  30.1 1.0 fusion.29
  31.2 0.0 all-gather.3.cloned.1.call-update
  31.2 0.0 reduce-scatter.2.cloned.1.call-start
  31.3 0.6 fusion.31
  31.8 22.3 %all-gather = f32[8,1,16]{2,1,0:T(1,128)S(1)} all-gather(f32[1,1,16]{2,1,0:T(1,128)S(1)} %get-tuple-element.9), channel_id=1, replica_groups=mesh['seq'=8,'head'=4] {'seq'}, dimensions={0}, use_global_device_ids=true | all-gather | bytes 576 | tf_op jit(solution)/shard_map/all_gather | solution.py:59
  54.1 0.1 select_reduce_fusion
  54.2 0.1 multiply_bitcast_fusion
  54.3 0.1 copy.71
  54.4 0.5 pad.clone
  54.9 0.5 pad.4.clone
  55.4 3.0 %copy.69 = bf16[1024,1024]{0,1:T(8,128)(2,1)S(1)} copy(bf16[1024,1024]{1,0:T(8,128)(2,1)} %param.11) | data formatting | bytes 4194304 | tf_op args[1]
  58.4 0.7 pad_maximum_fusion
  59.2 1.0 compare_and_fusion
  60.2 2.3 %fusion.37 = f32[4,256,256]{2,1,0:T(8,128)} fusion(bf16[4,256,128]{2,1,0:T(8,128)(2,1)S(1)} %bitcast.93, bf16[4,256,128]{2,1,0:T(8,128)(2,1)} %bitcast.98), kind=kOutput, calls=%fused_computation.82 | convolution fusion | flops 67108864 | bytes 1572864 | tf_op jit(solution)/shard_map/cin,cjn->cij/dot_general | solution.py:29
  62.4 21.0 %all-gather.3.cloned.1.call-done = bf16[8,16,64,128]{3,2,1,0:T(8,128)(2,1)} async-done(((bf16[1,16,64,128]{3,2,1,0:T(8,128)(2,1)}), bf16[8,16,64,128]{3,2,1,0:T(8,128)(2,1)}) %all-gather.3.cloned.1.call-update) | async-done | bytes 2097168 | tf_op jit(solution)/shard_map/all_gather | solution.py:70
  83.4 4.2 %fusion.18 = f32[16,1,64,128]{3,1,2,0:T(1,128)S(1)} fusion(f32[8,16,1,1]{0,2,3,1:T(1,128)S(1)} %copy.71, bf16[8,16,64,128]{3,2,1,0:T(8,128)(2,1)} %all-gather.3.cloned.1.call-done), kind=kOutput, calls=%fused_computation.29 | convolution fusion | flops 12582912 | bytes 2621952 | tf_op jit(solution)/shard_map/jh,jhpn->hpn/dot_general | solution.py:67
  87.7 3.0 %fusion.12 = f32[4,16,64,256]{3,2,1,0:T(8,128)S(1)} fusion(bf16[4,256,128,1]{2,1,3,0:T(8,128)(2,1)S(1)} %bitcast.92, f32[1,16,64,128]{3,2,1,0:T(8,128)S(1)} %get-tuple-element.6, f32[1,16,64,128]{3,2,1,0:T(8,128)S(1)} %get-tuple-element.7, f32[1,16,64,128]{3,2,1,0:T(8,128)} %get-tuple-element.8, f32[4]{0:T(128)S(1)} %copy-done.7, ...), kind=kOutput, calls=%fused_computation.23 | convolution fusion | flops 1613234176 | bytes 6553872 | tf_op jit(solution)/shard_map/cin,chpn->cihp/dot_general | solution.py:77
  90.7 5.6 %fusion.11 = f32[4,256,16,64]{1,3,2,0:T(8,128)S(1)} fusion(f32[4,16,64,256]{3,2,1,0:T(8,128)S(1)} %fusion.12, f32[4,256,16,64]{1,0,3,2:T(4,128)S(1)} %copy-done.1, f32[4,256,256]{2,1,0:T(8,128)S(1)} %copy-done.4, f32[16,4,256]{2,0,1:T(8,128)S(1)} %copy_bitcast_fusion, pred[4,256,256]{2,1,0:T(8,128)(4,1)S(1)} %copy-done.6, ...), kind=kOutput, calls=%fused_computation.16 | convolution fusion | flops 562036736 | bytes 16121920 | tf_op jit(solution)/shard_map/hcij,cjhp->cihp/dot_general | solution.py:36
  96.4 3.0 %copy.68 = f32[4,256,16,64]{1,0,3,2:T(4,128)S(1)} copy(f32[4,256,16,64]{1,3,2,0:T(8,128)S(1)} %fusion.11) | data formatting | bytes 8388608 | tf_op jit(solution)/shard_map/add | solution.py:80
  99.4 1.0 copy.78
  100.4 2.0 copy-done.2
  102.4 1.3 multiply_reduce_fusion
  103.7 5.7 %psum.7 = f32[1024]{0:T(1024)S(1)} all-reduce(f32[1024]{0:T(1024)S(1)} %multiply_reduce_fusion), channel_id=1, replica_groups=mesh['seq'=8,'head'=4] {'head'}, use_global_device_ids=true, to_apply=%region_6.7 | all-reduce | flops 1024 | bytes 8192 | tf_op jit(solution)/shard_map/psum | solution.py:83
  109.4 15.9 %convolution_convert_fusion = bf16[1024,4096]{1,0:T(8,128)(2,1)} fusion(bf16[1024,4096]{1,0:T(8,128)(2,1)} %param.19, f32[1024]{0:T(1024)S(1)} %copy-done.8, f32[1024]{0:T(1024)S(1)} %add_rsqrt_fusion, f32[1024,1024]{0,1:T(8,128)} %bitcast.95, bf16[1024,1024]{0,1:T(8,128)(2,1)S(1)} %copy.69), kind=kOutput, calls=%fused_computation.7 | convolution fusion | flops 8603566080 | bytes 23076864 | tf_op jit(solution)/shard_map/dot_general | solution.py:88
  125.3 0.0 reduce-scatter.2.cloned.1.call-update
  125.3 70.3 %reduce-scatter.2.cloned.1.call-done = bf16[256,4096]{1,0:T(8,128)(2,1)} async-done(((bf16[1024,4096]{1,0:T(8,128)(2,1)}), bf16[256,4096]{1,0:T(8,128)(2,1)}) %reduce-scatter.2.cloned.1.call-update) | async-done | bytes 2097168 | tf_op jit(solution)/shard_map/reduce_scatter | solution.py:87
  (33 shorter events, 0.2 us)
Async XLA Ops:
  6.5 53.6 %copy-start = (bf16[1024,128]{1,0:T(8,128)(2,1)S(1)}, bf16[1024,128]{1,0:T(8,128)(2,1)}, u32[]{:S(2)}) copy-start(bf16[1024,128]{1,0:T(8,128)(2,1)} %param.13) | copy-start | bytes 786436
  6.5 76.8 %all-gather.3.cloned.1.call-start = ((), (), s32[]{:S(2)}) async-start(), calls=%async_computation.1 | async-start | bytes 2359296 | tf_op jit(solution)/shard_map/all_gather | solution.py:70
  24.5 4.9 %copy-start.5 = (bf16[1024,128]{1,0:T(8,128)(2,1)S(1)}, bf16[1024,128]{1,0:T(8,128)(2,1)}, u32[]{:S(2)}) copy-start(bf16[1024,128]{1,0:T(8,128)(2,1)} %param.12) | copy-start | bytes 786436
  31.2 164.5 %reduce-scatter.2.cloned.1.call-start = ((), (), s32[]{:S(2)}) async-start(), calls=%async_computation.2 | async-start | bytes 10485760 | tf_op jit(solution)/shard_map/reduce_scatter | solution.py:87
  60.2 27.5 %copy-start.7 = (f32[4]{0:T(128)S(1)}, f32[4]{0:T(128)}, u32[]{:S(2)}) copy-start(f32[4]{0:T(128)} %pad.4.clone) | copy-start | bytes 52
  83.4 7.3 %copy-start.1 = (f32[4,256,16,64]{1,0,3,2:T(4,128)S(1)}, f32[4,256,16,64]{1,0,3,2:T(4,128)}, u32[]{:S(2)}) copy-start(f32[4,256,16,64]{1,0,3,2:T(4,128)} %reshape.272) | copy-start | bytes 12582916
  83.4 7.3 %copy-start.3 = (bf16[4,256,16,64]{1,0,3,2:T(4,128)(2,1)S(1)}, bf16[4,256,16,64]{1,0,3,2:T(4,128)(2,1)}, u32[]{:S(2)}) copy-start(bf16[4,256,16,64]{1,0,3,2:T(4,128)(2,1)} %get-tuple-element.13) | copy-start | bytes 6291460
  83.4 7.3 %copy-start.4 = (f32[4,256,256]{2,1,0:T(8,128)S(1)}, f32[4,256,256]{2,1,0:T(8,128)}, u32[]{:S(2)}) copy-start(f32[4,256,256]{2,1,0:T(8,128)} %fusion.37) | copy-start | bytes 3145732
  83.4 7.3 %copy-start.6 = (pred[4,256,256]{2,1,0:T(8,128)(4,1)S(1)}, pred[4,256,256]{2,1,0:T(8,128)(4,1)}, u32[]{:S(2)}) copy-start(pred[4,256,256]{2,1,0:T(8,128)(4,1)} %compare_and_fusion) | copy-start | bytes 786436
  83.4 7.3 %copy-start.9 = (f32[16]{0:T(128)S(1)}, f32[16]{0:T(128)}, u32[]{:S(2)}) copy-start(f32[16]{0:T(128)} %param.17) | copy-start | bytes 196
  100.4 2.0 copy-start.2
  100.4 9.0 %copy-start.8 = (f32[1024]{0:T(1024)S(1)}, f32[1024]{0:T(1024)}, u32[]{:S(2)}) copy-start(f32[1024]{0:T(1024)} %param.18) | copy-start | bytes 12292
Sparse Core Ops, SparseCore 0:
  31.3 52.0 all-gather.2
  125.4 70.1 reduce-scatter.1
where the time goes:
time: 203 us; the launch traced here: 202 us
  waiting for transfers between devices  91.4 us (45%)
  matrix products  31.7 us (16%)
  blocking collectives  27.9 us (14%)
  local copies, waits for them, and re-layouts  20.8 us (10%)
  other arithmetic  17 us (8%)
  between operations  13.6 us (7%)
    reduce_scatter x1, waiting for transfers between devices, local(): lax.psum_scatter(jnp.dot(hidden, out_weight, preferred_element_type=jnp.f...  70.3 us
    all_gather x1, blocking collectives, local(): decays = lax.all_gather(product[None], 'seq', axis=0, tiled=True)  22.3 us
    all_gather x1, waiting for transfers between devices, local(): lax.all_gather(running[None].astype(jnp.bfloat16), 'seq', axis=0, tiled=T...  21 us
    dot_general x1, matrix products, local(): jnp.dot(hidden, out_weight, preferred_element_type=jnp.float32)  15.9 us
    convert_element_type x2, local copies, waits for them, and re-layouts, local(): scaled = (raw_values.astype(jnp.float32) * step_scale).astype(jnp.bfloat16)  9.75 us
    unnamed x24, local copies, waits for them, and re-layouts  6.13 us
    psum x1, blocking collectives, local(): squared_values = lax.psum(jnp.sum(gated * gated, axis=1), 'head')  5.67 us
    dot_general x1, matrix products, local(): jnp.einsum('hcij,cjhp->cihp', scores, scaled, preferred_element_type=jnp....  5.64 us
  transfers between devices with their start and end apart: 2, of which 2 were waited for; matrix products, arithmetic and copies ran while one was open for 4% of the time, Pallas kernels for 0%

commit v1 on v0

v1 whole, which is shorter than its diff:
```python
import functools

import jax
import jax.numpy as jnp
from jax import lax
from jax.experimental import pallas as pl
from jax.experimental.pallas import tpu as pltpu
from jax.sharding import PartitionSpec as P


SPAN = 256
LANES = 128
LOG2E = 1.4426950408889634
F32 = jnp.float32
BF16 = jnp.bfloat16
PARAMS = pltpu.CompilerParams(vmem_limit_bytes=24 << 20)
CUTS = (1, 3, 4, 4, 2, 2)


def block_of(place, k, teams, i):
    team = (place[0] // 2 + k) % teams
    half = place[0] % 2
    return 2 * team + (half if i == 0 else 1 - half)


def block_cumsum(v):
    pos = lax.broadcasted_iota(jnp.int32, v.shape, 1) % SPAN
    k = 1
    while k < SPAN:
        v = v + jnp.where(pos >= k, pltpu.roll(v, k, 1), 0.0)
        k *= 2
    return v


def prep(dt, rate_ref, resets):
    step = dt.astype(F32) / 16.0
    scale = jnp.minimum(step, 1.0)
    row = lax.broadcasted_iota(jnp.int32, step.shape, 0)
    rate = jnp.zeros(step.shape, F32)
    for h in range(step.shape[0]):
        rate = jnp.where(row == h, rate_ref[h], rate)
    cum = block_cumsum((-LOG2E * rate) * step)
    count = block_cumsum(jnp.broadcast_to(resets.astype(F32), (8, resets.shape[1])))
    return scale, cum, count


def halves(first, second, shape, width):
    lane = lax.broadcasted_iota(jnp.int32, shape, 1) % LANES
    return jnp.where(lane < width, first, second)


def state_kernel(dt_ref, rate_ref, resets_ref, b_ref, x_ref, pay_ref, start_ref, reach_ref, w_s, bt_s, thr_s, *, pairs, width):
    blocks = start_ref.shape[0]
    state = b_ref.shape[1]

    @pl.when(pl.program_id(0) == 0)
    def _():
        scale, cum, count = prep(dt_ref[...], rate_ref, resets_ref[...])
        heads = cum.shape[0]
        for b in range(blocks):
            cols = slice(b * SPAN, (b + 1) * SPAN)
            c, n = cum[:, cols], count[:1, cols]
            end, last = c[:, SPAN - 1 :], n[:, SPAN - 1 :]
            w_s[:, cols] = jnp.where(n == last, jnp.exp2(end - c), 0.0) * scale[:, cols]
            through = jnp.where(last == 0.0, jnp.exp2(end), 0.0)
            thr_s[:, b * LANES : (b + 1) * LANES] = jnp.broadcast_to(through, (heads, LANES))
        bt_s[...] = b_ref[...].astype(F32).T

    own = pl.ds(pl.multiple_of(pl.program_id(0) * 2 * pairs, 2 * pairs), 2 * pairs)
    for i in range(pairs):
        lanes = slice(i * LANES, (i + 1) * LANES)
        running = jnp.zeros((state, LANES), F32)
        product = jnp.ones((1, LANES), F32)
        for b in range(blocks):
            cols = slice(b * SPAN, (b + 1) * SPAN)
            start_ref[b, :, lanes] = running.astype(BF16)
            reach_ref[b, :, lanes] = jnp.broadcast_to(product, (8, LANES))
            x = x_ref[cols, lanes]
            parts = []
            for k in range(2):
                row = w_s[own, cols][2 * i + k : 2 * i + k + 1]
                left = (bt_s[:, cols] * row).astype(BF16)
                parts.append(jnp.dot(left, x, preferred_element_type=F32))
            fresh = halves(parts[0], parts[1], (state, LANES), width)
            thr = thr_s[own, b * LANES : (b + 1) * LANES]
            thr = halves(thr[2 * i : 2 * i + 1], thr[2 * i + 1 : 2 * i + 2], (1, LANES), width)
            running = thr * running + fresh
            product = product * thr
        high = product.astype(BF16).astype(F32)
        mid = (product - high).astype(BF16).astype(F32)
        low = product - high - mid
        row = lax.broadcasted_iota(jnp.int32, (16, LANES), 0)
        tail = jnp.where(row == 0, high, jnp.where(row == 1, mid, jnp.where(row == 2, low, 0.0)))
        pay_ref[i, :state, :] = running.astype(BF16)
        pay_ref[i, state:, :] = tail.astype(BF16)


def states(dt, rate, resets, bmat, xs, blocks, width, pairs=4):
    tokens, channels = xs.shape
    heads, state = dt.shape[0], bmat.shape[1]
    count = channels // LANES
    whole = lambda *shape: pl.BlockSpec(shape, lambda i: (0,) * len(shape))
    return pl.pallas_call(
        functools.partial(state_kernel, pairs=pairs, width=width),
        grid=(count // pairs,),
        in_specs=[
            whole(heads, tokens),
            pl.BlockSpec(memory_space=pltpu.SMEM),
            whole(1, tokens),
            whole(tokens, state),
            pl.BlockSpec((tokens, pairs * LANES), lambda i: (0, i)),
        ],
        out_specs=[
            pl.BlockSpec((pairs, state + 16, LANES), lambda i: (i, 0, 0)),
            pl.BlockSpec((blocks, state, pairs * LANES), lambda i: (0, 0, i)),
            pl.BlockSpec((blocks, 8, pairs * LANES), lambda i: (0, 0, i)),
        ],
        out_shape=[
            jax.ShapeDtypeStruct((count, state + 16, LANES), BF16),
            jax.ShapeDtypeStruct((blocks, state, channels), BF16),
            jax.ShapeDtypeStruct((blocks, 8, channels), F32),
        ],
        scratch_shapes=[
            pltpu.VMEM((heads, tokens), F32),
            pltpu.VMEM((state, tokens), F32),
            pltpu.VMEM((heads, blocks * LANES), F32),
        ],
        cost_estimate=pl.CostEstimate(flops=4 * tokens * channels * state, bytes_accessed=4 << 20, transcendentals=tokens * heads),
        compiler_params=PARAMS,
        name="states",
    )(dt, rate, resets, bmat, xs)


def prefix_kernel(pay_ref, out_ref):
    shards, state = out_ref.shape[:2]
    running = jnp.zeros(out_ref.shape[1:], F32)
    for s in range(shards):
        out_ref[s] = running.astype(BF16)
        tail = pay_ref[s, state:, :].astype(F32)
        decay = tail[0:1] + tail[1:2] + tail[2:3]
        running = decay * running + pay_ref[s, :state, :].astype(F32)


def prefix(pay):
    shards, rows, lanes = pay.shape
    return pl.pallas_call(
        prefix_kernel,
        out_shape=jax.ShapeDtypeStruct((shards, rows - 16, lanes), BF16),
        cost_estimate=pl.CostEstimate(flops=shards * rows * lanes * 2, bytes_accessed=1 << 19, transcendentals=0),
        compiler_params=PARAMS,
        name="prefix",
    )(pay)


def intra_kernel(list_ref, dt_ref, rate_ref, resets_ref, skip_ref, b_ref, c_ref, x_ref, g_ref, base_ref, carry_ref, *, width):
    scale, cum, count = prep(dt_ref[...], rate_ref, resets_ref[...])
    heads = cum.shape[0]
    rows = cum - jnp.log2(scale)
    start = jnp.where(count[:1] == 0.0, jnp.exp2(cum), 0.0)
    stack = [cum, start, count, jnp.zeros((LANES - 2 * heads - 8, SPAN), F32)]
    flipped = jnp.concatenate(stack, axis=0).T
    dots = lax.dot_general(c_ref[...], b_ref[...], (((1,), (1,)), ((), ())), preferred_element_type=F32)
    i = lax.broadcasted_iota(jnp.int32, (SPAN, SPAN), 0)
    j = lax.broadcasted_iota(jnp.int32, (SPAN, SPAN), 1)
    linked = (flipped[:, 2 * heads : 2 * heads + 1] == count[:1]) & (j <= i)
    dots = jnp.where(linked, dots, 0.0)
    for pair in range(heads // 2):
        lanes = slice(pair * LANES, (pair + 1) * LANES)
        x = x_ref[:, lanes]
        left, right = [], []
        for k in range(2):
            h = 2 * pair + k
            gap = jnp.minimum(flipped[:, h : h + 1] - rows[h : h + 1], 0.0)
            left.append((jnp.exp2(gap) * dots).astype(BF16))
            zero = jnp.zeros_like(x)
            right.append(halves(x, zero, x.shape, width) if k == 0 else halves(zero, x, x.shape, width))
        intra = jnp.dot(jnp.concatenate(left, axis=1), jnp.concatenate(right, axis=0), preferred_element_type=F32)
        weight = halves(skip_ref[2 * pair], skip_ref[2 * pair + 1], (1, LANES), width)
        gate = g_ref[:, lanes].astype(F32)
        gate = gate / (1.0 + jnp.exp(-gate))
        base_ref[0, :, lanes] = (intra + weight * x.astype(F32)) * gate
        h = heads + 2 * pair
        carry = halves(flipped[:, h : h + 1], flipped[:, h + 1 : h + 2], x.shape, width)
        carry_ref[0, :, lanes] = (carry * gate).astype(BF16)


def intra(place, k, teams, dt, rate, resets, skip, bmat, cmat, xs, gate, width):
    _, channels = xs.shape
    heads, state = dt.shape[0], bmat.shape[1]
    count = 2
    at = lambda i, o: block_of(o, k, teams, 0) + i * (1 - 2 * (o[0] % 2))
    row = lambda n: pl.BlockSpec((SPAN, n), lambda i, o: (at(i, o), 0))
    out = pl.BlockSpec((1, SPAN, channels), lambda i, o: (i, 0, 0))
    return pl.pallas_call(
        functools.partial(intra_kernel, width=width),
        grid_spec=pltpu.PrefetchScalarGridSpec(
            num_scalar_prefetch=1,
            grid=(count,),
            in_specs=[
                pl.BlockSpec((heads, SPAN), lambda i, o: (0, at(i, o))),
                pl.BlockSpec(memory_space=pltpu.SMEM),
                pl.BlockSpec((1, SPAN), lambda i, o: (0, at(i, o))),
                pl.BlockSpec(memory_space=pltpu.SMEM),
                row(state),
                row(state),
                row(channels),
                row(channels),
            ],
            out_specs=[out, out],
        ),
        out_shape=[
            jax.ShapeDtypeStruct((count, SPAN, channels), F32),
            jax.ShapeDtypeStruct((count, SPAN, channels), BF16),
        ],
        cost_estimate=pl.CostEstimate(
            flops=8 * count * SPAN * SPAN * channels, bytes_accessed=count << 21, transcendentals=count * heads * SPAN * SPAN
        ),
        compiler_params=PARAMS,
        name="intra",
    )(place, dt, rate, resets, skip, bmat, cmat, xs, gate)


def finish_kernel(list_ref, c_ref, start_ref, reach_ref, in_ref, base_ref, carry_ref, gain_ref, hid_ref, sq_ref, total_s):
    step = pl.program_id(0)

    @pl.when(step == 0)
    def _():
        total_s[...] = jnp.zeros(total_s.shape, F32)

    full = []
    for q in range(in_ref.shape[0]):
        lanes = slice(q * LANES, (q + 1) * LANES)
        full.append((start_ref[0, :, lanes].astype(F32) + reach_ref[0, 0:1, lanes] * in_ref[q].astype(F32)).astype(BF16))
    inter = jnp.dot(c_ref[...], jnp.concatenate(full, axis=1), preferred_element_type=F32)
    gated = base_ref[0] + carry_ref[0].astype(F32) * inter
    square = gated * gated
    total = total_s[...]
    for q in range(in_ref.shape[0]):
        total = total + square[:, q * LANES : (q + 1) * LANES]
    total_s[...] = total
    hid_ref[0] = (gated * gain_ref[0:1, :]).astype(BF16)

    @pl.when(step == pl.num_programs(0) - 1)
    def _():
        sums = jnp.sum(total_s[...].T, axis=0, keepdims=True)
        sq_ref[0] = jnp.broadcast_to(sums, (8, SPAN))


def finish(place, k, teams, which, cmat, starts, reach, incoming, base, carry, gain, pairs=2):
    channels = base.shape[2]
    state = cmat.shape[1]
    wide = pairs * LANES
    at = lambda o: block_of(o, k, teams, which)
    part = pl.BlockSpec((1, SPAN, wide), lambda i, o: (which, 0, i))
    return pl.pallas_call(
        finish_kernel,
        grid_spec=pltpu.PrefetchScalarGridSpec(
            num_scalar_prefetch=1,
            grid=(channels // wide,),
            in_specs=[
                pl.BlockSpec((SPAN, state), lambda i, o: (at(o), 0)),
                pl.BlockSpec((1, state, wide), lambda i, o: (at(o), 0, i)),
                pl.BlockSpec((1, 8, wide), lambda i, o: (at(o), 0, i)),
                pl.BlockSpec((pairs, *incoming.shape[1:]), lambda i, o: (i, 0, 0)),
                part,
                part,
                pl.BlockSpec((1, wide), lambda i, o: (0, i)),
            ],
            out_specs=[
                pl.BlockSpec((1, SPAN, wide), lambda i, o: (0, 0, i)),
                pl.BlockSpec((1, 8, SPAN), lambda i, o: (0, 0, 0)),
            ],
            scratch_shapes=[pltpu.VMEM((SPAN, LANES), F32)],
        ),
        out_shape=[
            jax.ShapeDtypeStruct((1, SPAN, channels), BF16),
            jax.ShapeDtypeStruct((1, 8, SPAN), F32),
        ],
        cost_estimate=pl.CostEstimate(flops=2 * SPAN * state * channels, bytes_accessed=3 << 20, transcendentals=0),
        compiler_params=PARAMS,
        name="finish",
    )(place, cmat, starts, reach, incoming, base, carry, gain)


def product_kernel(a_ref, b_ref, wa_ref, wb_ref, out_ref):
    total = jnp.dot(a_ref[0], wa_ref[...], preferred_element_type=F32)
    total = total + jnp.dot(b_ref[0], wb_ref[...], preferred_element_type=F32)
    out_ref[...] = total.astype(out_ref.dtype)


def product(a, b, wa, wb, first, columns, dtype, tile=256):
    rows, depth = a.shape[1:]
    left = pl.BlockSpec((1, rows, depth), lambda i: (0, 0, 0))
    right = pl.BlockSpec((depth, tile), lambda i: (0, first // tile + i))
    return pl.pallas_call(
        product_kernel,
        grid=(columns // tile,),
        in_specs=[left, left, right, right],
        out_specs=pl.BlockSpec((rows, tile), lambda i: (0, i)),
        out_shape=jax.ShapeDtypeStruct((rows, columns), dtype),
        cost_estimate=pl.CostEstimate(flops=4 * rows * depth * columns, bytes_accessed=4 * depth * columns, transcendentals=0),
        compiler_params=PARAMS,
        name="product",
    )(a, b, wa, wb)


def close(square, own, parts, inner, out, first, tile=256):
    rows, columns = parts[0].shape
    at = lambda i: (0, first // tile + i)

    def body(*refs):
        sq_ref, own_ref = refs[:2]
        part_refs = refs[2 : 2 + len(parts)]
        out_ref = refs[-1]
        row = lax.rsqrt(sq_ref[...] / inner + 1e-05)
        total = own_ref[...]
        for part in part_refs:
            total = total + part[...].astype(F32)
        out_ref[...] = (total * row.T[:, 0:1]).astype(BF16)

    in_specs = [pl.BlockSpec(square.shape, lambda i: (0, 0)), pl.BlockSpec((rows, tile), at)]
    in_specs += [pl.BlockSpec((rows, tile), lambda i: (0, i))] * len(parts)
    args = [square, own, *parts]
    aliases = {}
    if out is not None:
        in_specs.append(pl.BlockSpec(memory_space=pl.ANY))
        args.append(out)
        aliases = {len(args) - 1: 0}
    return pl.pallas_call(
        body,
        grid=(columns // tile,),
        in_specs=in_specs,
        out_specs=pl.BlockSpec((rows, tile), at),
        out_shape=jax.ShapeDtypeStruct(own.shape, BF16),
        input_output_aliases=aliases,
        cost_estimate=pl.CostEstimate(flops=4 * rows * columns, bytes_accessed=8 * rows * columns, transcendentals=0),
        compiler_params=PARAMS,
        name="close",
    )(*args)


def exchange(slices):
    return lax.all_to_all(slices, "seq", 0, 0, tiled=True)


def local(xs, gate, bmat, cmat, dt, resets, decay_rate, skip, gain, weight, *, shards, group):
    tokens, channels = xs.shape
    heads, state = dt.shape[0], bmat.shape[1]
    width = channels // heads
    blocks = tokens // SPAN
    pairs = channels // LANES
    inner = float(group * channels)
    out_columns = weight.shape[1]
    me = lax.axis_index("head")
    teams = group // 2

    place = me.reshape(1).astype(jnp.int32)
    flags, gains = resets[None, :], gain[None, :]
    swap = [(i, i ^ 1) for i in range(group)]
    weight_b = lax.ppermute(weight, "head", swap)

    xs, gate, bmat, cmat, dt, weight, weight_b = [
        pltpu.with_memory_space_constraint(a, pltpu.HBM) for a in (xs, gate, bmat, cmat, dt, weight, weight_b)
    ]

    def after(value, *others):
        return lax.optimization_barrier((value, *others))[0]

    def inside(k, when):
        parts = intra(when, k, teams, dt, decay_rate, flags, skip, bmat, cmat, xs, gate, width)
        return [pltpu.with_memory_space_constraint(a, pltpu.HBM) for a in parts]

    payload, starts, reach = states(dt, decay_rate, flags, bmat, xs, blocks, width)
    rows = state + 16
    cut = channels // shards
    plain = shards == pairs
    if not plain:
        payload = payload.transpose(1, 0, 2).reshape(rows, shards, cut).transpose(1, 0, 2)
    gathered = exchange(payload)
    early = after(place, payload)
    locals_ = {k: inside(k, early) for k in range(1, teams)}
    prefixes = prefix(gathered)
    incoming = exchange(prefixes)
    locals_[0] = inside(0, after(place, prefixes))
    if not plain:
        incoming = incoming.transpose(1, 0, 2).reshape(state, pairs, LANES).transpose(1, 0, 2)

    def pair_of(k, when):
        done = []
        for which in (1, 0):
            hidden, sq = finish(when, k, teams, which, cmat, starts, reach, incoming, *locals_[k], gains)
            done.append((hidden, sq[0]))
        other = lax.ppermute(done[0][0], "head", swap)
        square = done[1][1] + lax.ppermute(done[0][1], "head", swap)
        return done[1][0], other, square

    received = []
    squares = []
    last = place
    unit = out_columns // sum(CUTS)
    for k in [*range(1, teams), 0]:
        hidden, other, square = pair_of(k, last)
        if k:
            send = [(i, (i + 2 * k) % group) for i in range(group)]
            squares.append(lax.ppermute(square, "head", send))
            first = 0
            chunks = []
            for n in CUTS:
                part = product(hidden, other, weight, weight_b, first, n * unit, BF16)
                hidden, part = lax.optimization_barrier((hidden, part))
                chunks.append(lax.ppermute(part, "head", send))
                first += n * unit
            last = after(place, part)
            received.append(chunks)
        else:
            squares.append(square)
            own = product(hidden, other, weight, weight_b, 0, out_columns, F32)
    square = sum(squares[1:], squares[0])
    out, first = None, 0
    for c, n in enumerate(CUTS):
        parts = [r[c] for r in received]
        out = close(square, own, parts, inner, out, first)
        if c + 1 < len(CUTS):
            for r in received:
                out, r[c + 1] = lax.optimization_barrier((out, r[c + 1]))
        first += n * unit
    return out


def solution(mesh):
    in_specs = (
        P("seq", "head"),
        P("seq", "head"),
        P("seq", None),
        P("seq", None),
        P("head", "seq"),
        P("seq"),
        P("head"),
        P("head"),
        P("head"),
        P("head", None),
    )
    out_specs = P(("seq", "head"), None)
    body = functools.partial(local, shards=mesh.shape["seq"], group=mesh.shape["head"])

    return jax.shard_map(body, mesh=mesh, in_specs=in_specs, out_specs=out_specs, check_vma=False)
```

time: 203 us -> 127 us (0.63)
  waiting for transfers between devices: 91.4 us -> 19.9 us
  Pallas kernels: 0 us -> 70 us
  matrix products: 31.7 us -> 0 us
  other arithmetic: 17 us -> 0.01 us
  local copies, waits for them, and re-layouts: 20.8 us -> 6.04 us
  between operations: 13.6 us -> 0.22 us
  starting transfers between devices: 0.04 us -> 12.3 us
  blocking collectives: 27.9 us -> 17.6 us
    reduce_scatter x1 -> x0, waiting for transfers between devices: 70.3 us -> none  [local(): lax.psum_scatter(jnp.dot(hidden, out_weight, preferred_element_type=jnp.f...]
    pallas_call x0 -> x21, Pallas kernels: none -> 70 us  [the longest x7 31.6 us: product(): pl.pallas_call(product_kernel, grid=(columns // tile,), in_specs=[left, l...]
    dot_general x6 -> x0, matrix products: 31.7 us -> none  [the longest x1 15.9 us: local(): jnp.dot(hidden, out_weight, preferred_element_type=jnp.float32)]
    all_gather x1 -> x0, blocking collectives: 22.3 us -> none  [local(): decays = lax.all_gather(product[None], 'seq', axis=0, tiled=True)]
    all_gather x1 -> x0, waiting for transfers between devices: 21 us -> none  [local(): lax.all_gather(running[None].astype(jnp.bfloat16), 'seq', axis=0, tiled=T...]
    ppermute x0 -> x12, waiting for transfers between devices: none -> 19.9 us  [the longest x6 18.4 us: local(): chunks.append(lax.ppermute(part, 'head', send))]
    all_to_all x0 -> x1, blocking collectives: none -> 17.6 us  [exchange(): return lax.all_to_all(slices, 'seq', 0, 0, tiled=True)]
    convert_element_type x2 -> x0, local copies, waits for them, and re-layouts: 9.75 us -> none  [local(): scaled = (raw_values.astype(jnp.float32) * step_scale).astype(jnp.bfloat16)]
  transfers between devices with their start and end apart: 2 -> 13, of which waited for: 2 -> 3; matrix products, arithmetic and copies ran while one was open for 4% -> 0% of each run, Pallas kernels for 0% -> 38%
where the time goes in v1:
time: 127 us; the launch traced here: 126 us
  Pallas kernels  70 us (55%)
  waiting for transfers between devices  19.9 us (16%)
  blocking collectives  17.6 us (14%)
  starting transfers between devices  12.3 us (10%)
  local copies, waits for them, and re-layouts  6.04 us (5%)
    pallas_call x7, Pallas kernels, product(): pl.pallas_call(product_kernel, grid=(columns // tile,), in_specs=[left, l...  31.6 us
    ppermute x6, waiting for transfers between devices, local(): chunks.append(lax.ppermute(part, 'head', send))  18.4 us
    all_to_all x1, blocking collectives, exchange(): return lax.all_to_all(slices, 'seq', 0, 0, tiled=True)  17.6 us
    pallas_call x2, Pallas kernels, intra(): pl.pallas_call(functools.partial(intra_kernel, width=width), grid_spec=pl...  12.3 us
    pallas_call x4, Pallas kernels, finish(): pl.pallas_call(finish_kernel, grid_spec=pltpu.PrefetchScalarGridSpec(num_...  11.9 us
    pallas_call x6, Pallas kernels, close(): pl.pallas_call(body, grid=(columns // tile,), in_specs=in_specs, out_spec...  9.83 us
    ppermute x6, starting transfers between devices, local(): chunks.append(lax.ppermute(part, 'head', send))  6.14 us
    unnamed x20, local copies, waits for them, and re-layouts  6.04 us
  transfers between devices with their start and end apart: 13, of which 3 were waited for; matrix products, arithmetic and copies ran while one was open for 0% of the time, Pallas kernels for 38%

profile of v1, /device:TPU:0, one launch (start us, length us, event | category | flops | bytes accessed | tf_op | source)
XLA Modules:
  0.0 126.1 jit_solution(10630511179761065345)
XLA Ops:
  0.0 0.5 collective-permute-start.3
  0.5 0.7 copy-done.5
  1.2 0.7 copy-done.7
  1.8 3.6 %states.1 = (bf16[8,144,128]{2,1,0:T(8,128)(2,1)S(1)}, bf16[4,128,1024]{2,1,0:T(8,128)(2,1)S(1)}, f32[4,8,1024]{2,1,0:T(8,128)S(1)}) custom-call(s32[16,1024]{1,0:T(8,128)} %dt_ref.5, f32[16]{0:T(128)S(1)} %copy-done.7, s32[1,1024]{1,0:T(1,128)S(1)} %bitcast.15, bf16[1024,128]{1,0:T(8,128)(2,1)} %b_ref.5, bf16[1024,1024]{1,0:T(8,128)(2,1)} %x_ref.5), custom_call_target="tpu_custom_call" | custom-call | flops 536870912 | bytes 4194304 | tf_op jit(solution)/shard_map/states/pallas_call | solution.py:103
  5.5 17.6 %all_to_all.10.pay_ref = bf16[8,144,128]{2,1,0:T(8,128)(2,1)S(1)} all-to-all(bf16[8,144,128]{2,1,0:T(8,128)(2,1)S(1)} %get-tuple-element.46), channel_id=1, replica_groups=mesh['seq'=8,'head'=4] {'seq'}, dimensions={0} | all-to-all | bytes 589824 | tf_op jit(solution)/shard_map/all_to_all | solution.py:343
  23.1 0.8 prefix.1
  23.8 3.4 %all-to-all-start.1 = ((bf16[8,128,128]{2,1,0:T(8,128)(2,1)}), bf16[8,128,128]{2,1,0:T(8,128)(2,1)S(1)}, u32[]{:S(2)}, u32[]{:S(2)}) async-start(bf16[8,128,128]{2,1,0:T(8,128)(2,1)} %prefix.1), calls=%async_computation.1 | async-start | bytes 524288 | tf_op jit(solution)/shard_map/all_to_all | solution.py:343
  27.3 0.0 copy-start.4
  27.3 6.1 %intra.2 = (f32[2,256,1024]{2,1,0:T(8,128)S(1)}, bf16[2,256,1024]{2,1,0:T(8,128)(2,1)S(1)}) custom-call(s32[1]{0:T(128)} %bitcast.list_ref, s32[16,1024]{1,0:T(8,128)} %dt_ref.5, f32[16]{0:T(128)S(1)} %copy-done.8, s32[1,1024]{1,0:T(1,128)S(1)} %bitcast.16, f32[16]{0:T(128)S(1)} %copy-done.9, bf16[1024,128]{1,0:T(8,128)(2,1)} %b_ref.5, ...), custom_call_target="tpu_custom_call" | custom-call | flops 1073741824 | bytes 4194304 | tf_op jit(solution)/shard_map/intra/pallas_call | solution.py:194
  33.4 0.0 copy-start.1
  33.4 1.3 %copy-done.1 = f32[2,256,1024]{2,1,0:T(8,128)} copy-done((f32[2,256,1024]{2,1,0:T(8,128)}, f32[2,256,1024]{2,1,0:T(8,128)S(1)}, u32[]{:S(2)}) %copy-start.1) | copy-done | bytes 2097176
  34.8 1.0 copy-done.3
  35.7 0.0 all-to-all-done.1.in_ref
  35.7 3.0 %finish.5 = (bf16[1,256,1024]{2,1,0:T(8,128)(2,1)S(1)}, f32[1,8,256]{2,1,0:T(8,128)S(1)}) custom-call(s32[1]{0:T(128)} %bitcast.list_ref, bf16[1024,128]{1,0:T(8,128)(2,1)} %c_ref.11, bf16[4,128,1024]{2,1,0:T(8,128)(2,1)S(1)} %get-tuple-element.44.start_ref, f32[4,8,1024]{2,1,0:T(8,128)S(1)} %get-tuple-element.45.reach_ref, ...), custom_call_target="tpu_custom_call" | custom-call | flops 67108864 | bytes 3145728 | tf_op jit(solution)/shard_map/finish/pallas_call | solution.py:255
  38.8 0.1 collective-permute-start.2
  38.8 6.1 %intra.3 = (f32[2,256,1024]{2,1,0:T(8,128)S(1)}, bf16[2,256,1024]{2,1,0:T(8,128)(2,1)S(1)}) custom-call(s32[1]{0:T(128)} %bitcast.list_ref, s32[16,1024]{1,0:T(8,128)} %dt_ref.5, f32[16]{0:T(128)S(1)} %copy-done.8, s32[1,1024]{1,0:T(1,128)S(1)} %bitcast.17, f32[16]{0:T(128)S(1)} %copy-done.9, bf16[1024,128]{1,0:T(8,128)(2,1)} %b_ref.5, ...), custom_call_target="tpu_custom_call" | custom-call | flops 1073741824 | bytes 4194304 | tf_op jit(solution)/shard_map/intra/pallas_call | solution.py:194
  45.0 1.4 %copy-done = f32[2,256,1024]{2,1,0:T(8,128)} copy-done((f32[2,256,1024]{2,1,0:T(8,128)}, f32[2,256,1024]{2,1,0:T(8,128)S(1)}, u32[]{:S(2)}) %copy-start) | copy-done | bytes 2097176
  46.4 1.0 copy-done.2
  47.4 3.0 %finish.4 = (bf16[1,256,1024]{2,1,0:T(8,128)(2,1)S(1)}, f32[1,8,256]{2,1,0:T(8,128)S(1)}) custom-call(s32[1]{0:T(128)} %bitcast.list_ref, bf16[1024,128]{1,0:T(8,128)(2,1)} %c_ref.11, bf16[4,128,1024]{2,1,0:T(8,128)(2,1)S(1)} %get-tuple-element.44.start_ref, f32[4,8,1024]{2,1,0:T(8,128)S(1)} %get-tuple-element.45.reach_ref, ...), custom_call_target="tpu_custom_call" | custom-call | flops 67108864 | bytes 3145728 | tf_op jit(solution)/shard_map/finish/pallas_call | solution.py:255
  50.4 0.0 collective-permute-done.2.b_ref
  50.4 1.6 %product.7 = bf16[256,256]{1,0:T(8,128)(2,1)S(1)} custom-call(bf16[1,256,1024]{2,1,0:T(8,128)(2,1)S(1)} %get-tuple-element.58.a_ref, bf16[1,256,1024]{2,1,0:T(8,128)(2,1)S(1)} %collective-permute-done.2.b_ref, bf16[1024,4096]{1,0:T(8,128)(2,1)} %wa_ref.13, bf16[1024,4096]{1,0:T(8,128)(2,1)} %collective-permute-done.3.wb_ref), custom_call_target="tpu_custom_call" | custom-call | flops 268435456 | bytes 1048576 | tf_op jit(solution)/shard_map/product/pallas_call | solution.py:295
  52.0 3.4 %product.8 = bf16[256,768]{1,0:T(8,128)(2,1)S(1)} custom-call(bf16[1,256,1024]{2,1,0:T(8,128)(2,1)S(1)} %get-tuple-element.58.a_ref, bf16[1,256,1024]{2,1,0:T(8,128)(2,1)S(1)} %collective-permute-done.2.b_ref, bf16[1024,4096]{1,0:T(8,128)(2,1)} %wa_ref.13, bf16[1024,4096]{1,0:T(8,128)(2,1)} %collective-permute-done.3.wb_ref), custom_call_target="tpu_custom_call" | custom-call | flops 805306368 | bytes 3145728 | tf_op jit(solution)/shard_map/product/pallas_call | solution.py:295
  55.4 3.9 %product.9 = bf16[256,1024]{1,0:T(8,128)(2,1)S(1)} custom-call(bf16[1,256,1024]{2,1,0:T(8,128)(2,1)S(1)} %get-tuple-element.58.a_ref, bf16[1,256,1024]{2,1,0:T(8,128)(2,1)S(1)} %collective-permute-done.2.b_ref, bf16[1024,4096]{1,0:T(8,128)(2,1)} %wa_ref.13, bf16[1024,4096]{1,0:T(8,128)(2,1)} %collective-permute-done.3.wb_ref), custom_call_target="tpu_custom_call" | custom-call | flops 1073741824 | bytes 4194304 | tf_op jit(solution)/shard_map/product/pallas_call | solution.py:295
  59.3 3.9 %product.10 = bf16[256,1024]{1,0:T(8,128)(2,1)S(1)} custom-call(bf16[1,256,1024]{2,1,0:T(8,128)(2,1)S(1)} %get-tuple-element.58.a_ref, bf16[1,256,1024]{2,1,0:T(8,128)(2,1)S(1)} %collective-permute-done.2.b_ref, bf16[1024,4096]{1,0:T(8,128)(2,1)} %wa_ref.13, bf16[1024,4096]{1,0:T(8,128)(2,1)} %collective-permute-done.3.wb_ref), custom_call_target="tpu_custom_call" | custom-call | flops 1073741824 | bytes 4194304 | tf_op jit(solution)/shard_map/product/pallas_call | solution.py:295
  63.3 2.2 %product.11 = bf16[256,512]{1,0:T(8,128)(2,1)S(1)} custom-call(bf16[1,256,1024]{2,1,0:T(8,128)(2,1)S(1)} %get-tuple-element.58.a_ref, bf16[1,256,1024]{2,1,0:T(8,128)(2,1)S(1)} %collective-permute-done.2.b_ref, bf16[1024,4096]{1,0:T(8,128)(2,1)} %wa_ref.13, bf16[1024,4096]{1,0:T(8,128)(2,1)} %collective-permute-done.3.wb_ref), custom_call_target="tpu_custom_call" | custom-call | flops 536870912 | bytes 2097152 | tf_op jit(solution)/shard_map/product/pallas_call | solution.py:295
  65.4 2.2 %product.12 = bf16[256,512]{1,0:T(8,128)(2,1)S(1)} custom-call(bf16[1,256,1024]{2,1,0:T(8,128)(2,1)S(1)} %get-tuple-element.58.a_ref, bf16[1,256,1024]{2,1,0:T(8,128)(2,1)S(1)} %collective-permute-done.2.b_ref, bf16[1024,4096]{1,0:T(8,128)(2,1)} %wa_ref.13, bf16[1024,4096]{1,0:T(8,128)(2,1)} %collective-permute-done.3.wb_ref), custom_call_target="tpu_custom_call" | custom-call | flops 536870912 | bytes 2097152 | tf_op jit(solution)/shard_map/product/pallas_call | solution.py:295
  67.6 3.0 %finish.7 = (bf16[1,256,1024]{2,1,0:T(8,128)(2,1)S(1)}, f32[1,8,256]{2,1,0:T(8,128)S(1)}) custom-call(s32[1]{0:T(128)} %bitcast.list_ref, bf16[1024,128]{1,0:T(8,128)(2,1)} %c_ref.11, bf16[4,128,1024]{2,1,0:T(8,128)(2,1)S(1)} %get-tuple-element.44.start_ref, f32[4,8,1024]{2,1,0:T(8,128)S(1)} %get-tuple-element.45.reach_ref, ...), custom_call_target="tpu_custom_call" | custom-call | flops 67108864 | bytes 3145728 | tf_op jit(solution)/shard_map/finish/pallas_call | solution.py:255
  70.6 0.5 collective-permute-start.5
  71.1 0.1 collective-permute-start
  71.2 1.5 %collective-permute-done = f32[8,256]{1,0:T(8,128)S(1)} collective-permute-done((f32[8,256]{1,0:T(8,128)S(1)}, f32[8,256]{1,0:T(8,128)S(1)}, u32[]{:S(2)}, u32[]{:S(2)}) %collective-permute-start) | collective-permute-done | bytes 8224 | tf_op jit(solution)/shard_map/ppermute | solution.py:394
  72.7 1.5 %collective-permute-start.1 = (f32[8,256]{1,0:T(8,128)S(1)}, f32[8,256]{1,0:T(8,128)S(1)}, u32[]{:S(2)}, u32[]{:S(2)}) collective-permute-start(f32[8,256]{1,0:T(8,128)S(1)} %bitcast_add_fusion.1), channel_id=1, source_target_pairs={{0,2},{1,3},{2,0},{3,1},{4,6},{5,7},{6,4},{7,5},{8,10},{9,11},{10,... | collective-permute-start | bytes 24584 | tf_op jit(solution)/shard_map/ppermute | solution.py:405
  74.2 0.1 collective-permute-start.4
  74.3 0.5 collective-permute-start.11
  74.8 1.5 %collective-permute-start.6 = (bf16[256,256]{1,0:T(8,128)(2,1)S(1)}, bf16[256,256]{1,0:T(8,128)(2,1)S(1)}, u32[]{:S(2)}, u32[]{:S(2)}) collective-permute-start(bf16[256,256]{1,0:T(8,128)(2,1)S(1)} %product.7), channel_id=1, source_target_pairs={{0,2},{1,3},{2,0},{3,1},{4,6},{5,7},{6,4},{7,5},{8,10},{9,11},{10,... | collective-permute-start | bytes 393224 | tf_op jit(solution)/shard_map/ppermute | solution.py:411
  76.3 3.0 %finish.6 = (bf16[1,256,1024]{2,1,0:T(8,128)(2,1)S(1)}, f32[1,8,256]{2,1,0:T(8,128)S(1)}) custom-call(s32[1]{0:T(128)} %bitcast.list_ref, bf16[1024,128]{1,0:T(8,128)(2,1)} %c_ref.11, bf16[4,128,1024]{2,1,0:T(8,128)(2,1)S(1)} %get-tuple-element.44.start_ref, f32[4,8,1024]{2,1,0:T(8,128)S(1)} %get-tuple-element.45.reach_ref, ...), custom_call_target="tpu_custom_call" | custom-call | flops 67108864 | bytes 3145728 | tf_op jit(solution)/shard_map/finish/pallas_call | solution.py:255
  79.3 0.6 collective-permute-start.9
  79.9 1.5 %collective-permute-start.8 = (bf16[256,1024]{1,0:T(8,128)(2,1)S(1)}, bf16[256,1024]{1,0:T(8,128)(2,1)S(1)}, u32[]{:S(2)}, u32[]{:S(2)}) collective-permute-start(bf16[256,1024]{1,0:T(8,128)(2,1)S(1)} %product.9), channel_id=1, source_target_pairs={{0,2},{1,3},{2,0},{3,1},{4,6},{5,7},{6,4},{7,5},{8,10},{9,11},{10,... | collective-permute-start | bytes 1572872 | tf_op jit(solution)/shard_map/ppermute | solution.py:411
  81.4 4.9 %collective-permute-done.6.refs_2_ = bf16[256,256]{1,0:T(8,128)(2,1)S(1)} collective-permute-done((bf16[256,256]{1,0:T(8,128)(2,1)S(1)}, bf16[256,256]{1,0:T(8,128)(2,1)S(1)}, u32[]{:S(2)}, u32[]{:S(2)}) %collective-permute-start.6) | collective-permute-done | bytes 131104 | tf_op jit(solution)/shard_map/ppermute | solution.py:411
  86.3 0.5 collective-permute-start.7
  86.8 1.5 %collective-permute-start.10 = (bf16[256,512]{1,0:T(8,128)(2,1)S(1)}, bf16[256,512]{1,0:T(8,128)(2,1)S(1)}, u32[]{:S(2)}, u32[]{:S(2)}) collective-permute-start(bf16[256,512]{1,0:T(8,128)(2,1)S(1)} %product.11), channel_id=1, source_target_pairs={{0,2},{1,3},{2,0},{3,1},{4,6},{5,7},{6,4},{7,5},{8,10},{9,11},{10,... | collective-permute-start | bytes 786440 | tf_op jit(solution)/shard_map/ppermute | solution.py:411
  88.3 14.4 %product.13.refs_1_ = f32[256,4096]{1,0:T(8,128)S(1)} custom-call(bf16[1,256,1024]{2,1,0:T(8,128)(2,1)S(1)} %get-tuple-element.66.a_ref, bf16[1,256,1024]{2,1,0:T(8,128)(2,1)S(1)} %collective-permute-done.5.b_ref, bf16[1024,4096]{1,0:T(8,128)(2,1)} %wa_ref.13, bf16[1024,4096]{1,0:T(8,128)(2,1)} %collective-permute-done.3.wb_ref), custom_call_target="tpu_custom_call" | custom-call | flops 4294967296 | bytes 16777216 | tf_op jit(solution)/shard_map/product/pallas_call | solution.py:295
  102.7 0.9 close.6.refs_3_
  103.6 13.6 %collective-permute-done.7.refs_2_ = bf16[256,768]{1,0:T(8,128)(2,1)S(1)} collective-permute-done((bf16[256,768]{1,0:T(8,128)(2,1)S(1)}, bf16[256,768]{1,0:T(8,128)(2,1)S(1)}, u32[]{:S(2)}, u32[]{:S(2)}) %collective-permute-start.7) | collective-permute-done | bytes 393248 | tf_op jit(solution)/shard_map/ppermute | solution.py:411
  117.2 1.9 %close.7.refs_3_ = bf16[256,4096]{1,0:T(8,128)(2,1)} custom-call(f32[8,256]{1,0:T(8,128)S(1)} %fusion.refs_0_, f32[256,4096]{1,0:T(8,128)S(1)} %product.13.refs_1_, bf16[256,768]{1,0:T(8,128)(2,1)S(1)} %collective-permute-done.7.refs_2_, bf16[256,4096]{1,0:T(8,128)(2,1)} %close.6.refs_3_), custom_call_target="tpu_custom_call", output_to_operand_aliasing={{}: (3, {})} | custom-call | flops 786432 | bytes 1572864 | tf_op jit(solution)/shard_map/close/pallas_call | solution.py:329
  119.1 2.2 %close.8.refs_3_ = bf16[256,4096]{1,0:T(8,128)(2,1)} custom-call(f32[8,256]{1,0:T(8,128)S(1)} %fusion.refs_0_, f32[256,4096]{1,0:T(8,128)S(1)} %product.13.refs_1_, bf16[256,1024]{1,0:T(8,128)(2,1)S(1)} %collective-permute-done.8.refs_2_, bf16[256,4096]{1,0:T(8,128)(2,1)} %close.7.refs_3_), custom_call_target="tpu_custom_call", output_to_operand_aliasing={{}: (3, {})} | custom-call | flops 1048576 | bytes 2097152 | tf_op jit(solution)/shard_map/close/pallas_call | solution.py:329
  121.3 2.2 %close.9.refs_3_ = bf16[256,4096]{1,0:T(8,128)(2,1)} custom-call(f32[8,256]{1,0:T(8,128)S(1)} %fusion.refs_0_, f32[256,4096]{1,0:T(8,128)S(1)} %product.13.refs_1_, bf16[256,1024]{1,0:T(8,128)(2,1)S(1)} %collective-permute-done.9.refs_2_, bf16[256,4096]{1,0:T(8,128)(2,1)} %close.8.refs_3_), custom_call_target="tpu_custom_call", output_to_operand_aliasing={{}: (3, {})} | custom-call | flops 1048576 | bytes 2097152 | tf_op jit(solution)/shard_map/close/pallas_call | solution.py:329
  123.6 1.3 %close.10.refs_3_ = bf16[256,4096]{1,0:T(8,128)(2,1)} custom-call(f32[8,256]{1,0:T(8,128)S(1)} %fusion.refs_0_, f32[256,4096]{1,0:T(8,128)S(1)} %product.13.refs_1_, bf16[256,512]{1,0:T(8,128)(2,1)S(1)} %collective-permute-done.10.refs_2_, bf16[256,4096]{1,0:T(8,128)(2,1)} %close.9.refs_3_), custom_call_target="tpu_custom_call", output_to_operand_aliasing={{}: (3, {})} | custom-call | flops 524288 | bytes 1048576 | tf_op jit(solution)/shard_map/close/pallas_call | solution.py:329
  124.8 1.3 %close.11 = bf16[256,4096]{1,0:T(8,128)(2,1)} custom-call(f32[8,256]{1,0:T(8,128)S(1)} %fusion.refs_0_, f32[256,4096]{1,0:T(8,128)S(1)} %product.13.refs_1_, bf16[256,512]{1,0:T(8,128)(2,1)S(1)} %collective-permute-done.11.refs_2_, bf16[256,4096]{1,0:T(8,128)(2,1)} %close.10.refs_3_), custom_call_target="tpu_custom_call", output_to_operand_aliasing={{}: (3, {})} | custom-call | flops 524288 | bytes 1048576 | tf_op jit(solution)/shard_map/close/pallas_call | solution.py:329
  (22 shorter events, 0.1 us)
Async XLA Ops:
  0.0 27.3 %copy-start.8 = (f32[16]{0:T(128)S(1)}, f32[16]{0:T(128)}, u32[]{:S(2)}) copy-start(f32[16]{0:T(128)} %rate_ref.5) | copy-start | bytes 196
  0.0 27.3 %copy-start.9 = (f32[16]{0:T(128)S(1)}, f32[16]{0:T(128)}, u32[]{:S(2)}) copy-start(f32[16]{0:T(128)} %skip_ref.3) | copy-start | bytes 196
  0.0 50.4 %collective-permute-start.3 = (bf16[1024,4096]{1,0:T(8,128)(2,1)}, bf16[1024,4096]{1,0:T(8,128)(2,1)}, u32[]{:S(2)}, u32[]{:S(2)}) collective-permute-start(bf16[1024,4096]{1,0:T(8,128)(2,1)} %wa_ref.13), channel_id=1, source_target_pairs={{0,1},{1,0},{2,3},{3,2},{4,5},{5,4},{6,7},{7,6},{8,9},{9,8},{10,11... | collective-permute-start | bytes 25165832 | tf_op jit(solution)/shard_map/ppermute | solution.py:360
  0.5 0.7 copy-start.5
  1.2 0.7 copy-start.7
  1.8 25.4 %copy-start.6 = (s32[1024]{0:T(1024)S(1)}, s32[1024]{0:T(1024)}, u32[]{:S(2)}) copy-start(s32[1024]{0:T(1024)} %param.15) | copy-start | bytes 12292
  23.8 11.9 %all-to-all-start.1 = ((bf16[8,128,128]{2,1,0:T(8,128)(2,1)}), bf16[8,128,128]{2,1,0:T(8,128)(2,1)S(1)}, u32[]{:S(2)}, u32[]{:S(2)}) async-start(bf16[8,128,128]{2,1,0:T(8,128)(2,1)} %prefix.1), calls=%async_computation.1 | async-start | bytes 524288 | tf_op jit(solution)/shard_map/all_to_all | solution.py:343
  27.3 8.5 %copy-start.4 = (f32[1024]{0:T(1024)S(1)}, f32[1024]{0:T(1024)}, u32[]{:S(2)}) copy-start(f32[1024]{0:T(1024)} %param.18) | copy-start | bytes 12292
  33.4 1.3 %copy-start.1 = (f32[2,256,1024]{2,1,0:T(8,128)}, f32[2,256,1024]{2,1,0:T(8,128)S(1)}, u32[]{:S(2)}) copy-start(f32[2,256,1024]{2,1,0:T(8,128)S(1)} %get-tuple-element.48.base_ref) | copy-start | bytes 6291460
  34.8 1.0 copy-start.3
  38.8 11.6 %collective-permute-start.2 = (bf16[1,256,1024]{2,1,0:T(8,128)(2,1)S(1)}, bf16[1,256,1024]{2,1,0:T(8,128)(2,1)S(1)}, u32[]{:S(2)}, u32[]{:S(2)}) collective-permute-start(bf16[1,256,1024]{2,1,0:T(8,128)(2,1)S(1)} %get-tuple-element.53), channel_id=1, source_target_pairs={{0,1},{1,0},{2,3},{3,2},{4,5},{5,4},{6,7},{7,6},{8,9},{9,8},{10,11... | collective-permute-start | bytes 1572872 | tf_op jit(solution)/shard_map/ppermute | solution.py:393
  45.0 1.4 %copy-start = (f32[2,256,1024]{2,1,0:T(8,128)}, f32[2,256,1024]{2,1,0:T(8,128)S(1)}, u32[]{:S(2)}) copy-start(f32[2,256,1024]{2,1,0:T(8,128)S(1)} %get-tuple-element.62.base_ref) | copy-start | bytes 6291460
  46.4 1.0 copy-start.2
  70.6 16.2 %collective-permute-start.5 = (bf16[1,256,1024]{2,1,0:T(8,128)(2,1)S(1)}, bf16[1,256,1024]{2,1,0:T(8,128)(2,1)S(1)}, u32[]{:S(2)}, u32[]{:S(2)}) collective-permute-start(bf16[1,256,1024]{2,1,0:T(8,128)(2,1)S(1)} %get-tuple-element.67), channel_id=1, source_target_pairs={{0,1},{1,0},{2,3},{3,2},{4,5},{5,4},{6,7},{7,6},{8,9},{9,8},{10,11... | collective-permute-start | bytes 1572872 | tf_op jit(solution)/shard_map/ppermute | solution.py:393
  71.1 1.5 %collective-permute-start = (f32[8,256]{1,0:T(8,128)S(1)}, f32[8,256]{1,0:T(8,128)S(1)}, u32[]{:S(2)}, u32[]{:S(2)}) collective-permute-start(f32[8,256]{1,0:T(8,128)S(1)} %bitcast.19), channel_id=1, source_target_pairs={{0,1},{1,0},{2,3},{3,2},{4,5},{5,4},{6,7},{7,6},{8,9},{9,8},{10,11... | collective-permute-start | bytes 24584 | tf_op jit(solution)/shard_map/ppermute | solution.py:394
  72.7 6.6 %collective-permute-start.1 = (f32[8,256]{1,0:T(8,128)S(1)}, f32[8,256]{1,0:T(8,128)S(1)}, u32[]{:S(2)}, u32[]{:S(2)}) collective-permute-start(f32[8,256]{1,0:T(8,128)S(1)} %bitcast_add_fusion.1), channel_id=1, source_target_pairs={{0,2},{1,3},{2,0},{3,1},{4,6},{5,7},{6,4},{7,5},{8,10},{9,11},{10,... | collective-permute-start | bytes 24584 | tf_op jit(solution)/shard_map/ppermute | solution.py:405
  74.2 5.7 %collective-permute-start.4 = (f32[8,256]{1,0:T(8,128)S(1)}, f32[8,256]{1,0:T(8,128)S(1)}, u32[]{:S(2)}, u32[]{:S(2)}) collective-permute-start(f32[8,256]{1,0:T(8,128)S(1)} %bitcast.18), channel_id=1, source_target_pairs={{0,1},{1,0},{2,3},{3,2},{4,5},{5,4},{6,7},{7,6},{8,9},{9,8},{10,11... | collective-permute-start | bytes 24584 | tf_op jit(solution)/shard_map/ppermute | solution.py:394
  74.3 50.5 %collective-permute-start.11 = (bf16[256,512]{1,0:T(8,128)(2,1)S(1)}, bf16[256,512]{1,0:T(8,128)(2,1)S(1)}, u32[]{:S(2)}, u32[]{:S(2)}) collective-permute-start(bf16[256,512]{1,0:T(8,128)(2,1)S(1)} %product.12), channel_id=1, source_target_pairs={{0,2},{1,3},{2,0},{3,1},{4,6},{5,7},{6,4},{7,5},{8,10},{9,11},{10,... | collective-permute-start | bytes 786440 | tf_op jit(solution)/shard_map/ppermute | solution.py:411
  74.8 11.5 %collective-permute-start.6 = (bf16[256,256]{1,0:T(8,128)(2,1)S(1)}, bf16[256,256]{1,0:T(8,128)(2,1)S(1)}, u32[]{:S(2)}, u32[]{:S(2)}) collective-permute-start(bf16[256,256]{1,0:T(8,128)(2,1)S(1)} %product.7), channel_id=1, source_target_pairs={{0,2},{1,3},{2,0},{3,1},{4,6},{5,7},{6,4},{7,5},{8,10},{9,11},{10,... | collective-permute-start | bytes 393224 | tf_op jit(solution)/shard_map/ppermute | solution.py:411
  79.3 42.0 %collective-permute-start.9 = (bf16[256,1024]{1,0:T(8,128)(2,1)S(1)}, bf16[256,1024]{1,0:T(8,128)(2,1)S(1)}, u32[]{:S(2)}, u32[]{:S(2)}) collective-permute-start(bf16[256,1024]{1,0:T(8,128)(2,1)S(1)} %product.10), channel_id=1, source_target_pairs={{0,2},{1,3},{2,0},{3,1},{4,6},{5,7},{6,4},{7,5},{8,10},{9,11},{10,... | collective-permute-start | bytes 1572872 | tf_op jit(solution)/shard_map/ppermute | solution.py:411
  79.9 39.2 %collective-permute-start.8 = (bf16[256,1024]{1,0:T(8,128)(2,1)S(1)}, bf16[256,1024]{1,0:T(8,128)(2,1)S(1)}, u32[]{:S(2)}, u32[]{:S(2)}) collective-permute-start(bf16[256,1024]{1,0:T(8,128)(2,1)S(1)} %product.9), channel_id=1, source_target_pairs={{0,2},{1,3},{2,0},{3,1},{4,6},{5,7},{6,4},{7,5},{8,10},{9,11},{10,... | collective-permute-start | bytes 1572872 | tf_op jit(solution)/shard_map/ppermute | solution.py:411
  86.3 30.9 %collective-permute-start.7 = (bf16[256,768]{1,0:T(8,128)(2,1)S(1)}, bf16[256,768]{1,0:T(8,128)(2,1)S(1)}, u32[]{:S(2)}, u32[]{:S(2)}) collective-permute-start(bf16[256,768]{1,0:T(8,128)(2,1)S(1)} %product.8), channel_id=1, source_target_pairs={{0,2},{1,3},{2,0},{3,1},{4,6},{5,7},{6,4},{7,5},{8,10},{9,11},{10,... | collective-permute-start | bytes 1179656 | tf_op jit(solution)/shard_map/ppermute | solution.py:411
  86.8 36.8 %collective-permute-start.10 = (bf16[256,512]{1,0:T(8,128)(2,1)S(1)}, bf16[256,512]{1,0:T(8,128)(2,1)S(1)}, u32[]{:S(2)}, u32[]{:S(2)}) collective-permute-start(bf16[256,512]{1,0:T(8,128)(2,1)S(1)} %product.11), channel_id=1, source_target_pairs={{0,2},{1,3},{2,0},{3,1},{4,6},{5,7},{6,4},{7,5},{8,10},{9,11},{10,... | collective-permute-start | bytes 786440 | tf_op jit(solution)/shard_map/ppermute | solution.py:411
